TPU v7x, 32 devices: a whole 2x2x4 slice. The times are simulated.
32 devices in a mesh: gx: 8 (over z, y), gy: 4 (over x, core).
Axes of the slice: x: 2, y: 2, z: 4, core: 2. Of those that a mesh axis runs over, the one named last changes fastest.
Arguments:
- populations: float32 [27, 16, 32, 128], P(None, 'gx', 'gy'), as said below
- relax: float32 [27], replicated, may hold values from 0.6 to 1.9
- solid: int32 [16, 32, 128], P('gx', 'gy'), may hold values 0 or 1
- wall_cell: int32 [8, 4, 256], P('gx', 'gy'), may hold values from 0 to 2047, as said below
- wall_normal: int32 [8, 4, 256], P('gx', 'gy'), may hold values from 0 to 5
- wall_count: int32 [8, 4], P('gx', 'gy'), may hold values from 1 to 256, as said below
- sample_ref: int32 [8, 4, 256], P('gx', 'gy'), may hold values from 0 to 255, each once within a row
- stencil_cell: int32 [8, 4, 8, 256], P('gx', 'gy'), may hold values from 0 to 2047, as said below
- stencil_weight: float32 [8, 4, 8, 256], P('gx', 'gy'), may hold values from 0 to 1, as said below
Outputs:
- read: float32 [27, 16, 32, 128], P(None, 'gx', 'gy')
Inputs may be any that keep to these rules, and one draw needn't show every extreme that they name: `populations`: positive everywhere. `wall_cell`: the 256 entries of one device are distinct local cells. Slots 0 to wall_count - 1 of a device are live; some device has all 256 live. `stencil_cell`: the eight corners of a unit cube of the owner's local cells, wrapping along z only. `stencil_weight`: nonnegative trilinear weights, summing to one over the eight corners.
All inputs are finite; a program needn't handle non-finite values. No bound on the sum of `solid` on one device may be relied on, other than what follows from the above.
Results may differ from a plain program's by a relative error of at most 0.0003.
Values sent between devices are 32-bit elements; how exact they have to be, the bound alone decides.
No kernel may reach another device: no remote copies, remote signals or barrier semaphores. Data moves between devices by JAX's collectives and lax.ppermute only.
A program may use at most 64 MiB of HBM per device.

v0:
```python
import jax
import jax.numpy as jnp
from jax import lax
from jax.experimental import pallas as pl
from jax.experimental.pallas import tpu as pltpu
from jax.sharding import PartitionSpec as P


wall_ratio = (1.0 / 9.0) ** (1.0 / 7.0)
LANES = 128
ROWS = 8
RHO, VEL, PLANES = 27, 28, 31
REF, AXIS, SOLID = 0, 1, 2
FACE = 16
HBM = pl.BlockSpec(memory_space=pltpu.HBM)
VMEM = pl.BlockSpec(memory_space=pltpu.VMEM)
THROUGH = ("normal", "ref", "relax")
COVER = 4 * 10**9
GRANT = 4 * 1024 * 1024


def direction(a, b, c):
    return 9 * a + 3 * b + c


def up(n):
    return -(-n // ROWS) * ROWS


def equilibria(density, velocity, wanted):
    ux, uy, uz = velocity
    rest = density * (1.0 - 1.5 * (ux * ux + uy * uy + uz * uz))
    out = {}
    for i in wanted:
        if i in out:
            continue
        step = (i // 9 - 1, i // 3 % 3 - 1, i % 3 - 1)
        along = None
        for s, u in zip(step, (ux, uy, uz)):
            if s:
                along = (u if s > 0 else -u) if along is None else (along + u if s > 0 else along - u)
        if along is None:
            out[i] = rest
            continue
        linear = density * along
        square = rest + 4.5 * (linear * along)
        out[i] = square + 3.0 * linear
        if 26 - i in wanted:
            out[26 - i] = square - 3.0 * linear
    return out


def along_axes(values, triple):
    for stride in (1, 3, 9):
        fresh = list(values)
        for i in range(27):
            if i // stride % 3 == 0:
                fresh[i], fresh[i + stride], fresh[i + 2 * stride] = triple(
                    values[i], values[i + stride], values[i + 2 * stride]
                )
        values = fresh
    return values


def relaxed(pops, keep):
    single = (1.0 / 6.0, 2.0 / 3.0, 1.0 / 6.0)
    weight = [single[i // 9] * single[i // 3 % 3] * single[i % 3] for i in range(27)]

    def raw(m, z, p):
        s = m + p
        return s + z, p - m, s

    def undo(m0, m1, m2):
        return m2 - m1, m0 - m2, m1 + m2

    moment = along_axes([w * p for w, p in zip(weight, pops)], raw)
    density = moment[0]
    inv = 1.0 / density
    vel = [moment[9] * inv, moment[3] * inv, moment[1] * inv]
    first = [moment[9], moment[3], moment[1]]
    second = [4.5 * (j * u) for j, u in zip(first, vel)]
    rest = density - (1.0 / 3.0) * (second[0] + second[1] + second[2])
    mu, nu, ka = (1.0, 0.0, 1.0 / 3.0), (0.0, 1.0 / 3.0, 0.0), (1.0 / 3.0, 0.0, 1.0 / 3.0)
    cross = {}
    kept = []
    for i in range(27):
        p = (i // 9, i // 3 % 3, i % 3)
        eq = None
        terms = [(mu[p[0]] * mu[p[1]] * mu[p[2]], rest)]
        for d in range(3):
            o, q = [e for e in range(3) if e != d]
            terms.append((3.0 * nu[p[d]] * mu[p[o]] * mu[p[q]], first[d]))
            terms.append((ka[p[d]] * mu[p[o]] * mu[p[q]], second[d]))
            factor = 9.0 * nu[p[o]] * nu[p[q]] * mu[p[d]]
            if factor:
                if d not in cross:
                    cross[d] = first[o] * vel[q]
                terms.append((factor, cross[d]))
        for f, t in terms:
            if f:
                t = t if abs(f - 1.0) < 1e-12 else f * t
                eq = t if eq is None else eq + t
        dev = moment[i] if eq is None else moment[i] - eq
        kept.append(keep[i] * dev)
    back = (3.0, 1.5, 3.0)
    kept = along_axes(kept, undo)
    kept = [back[i // 9] * back[i // 3 % 3] * back[i % 3] * k for i, k in enumerate(kept)]
    return density, vel, kept


def lanes_of(table, index):
    return jnp.take_along_axis(table, index, axis=1, mode="promise_in_bounds")


def number_kernel(out):
    out[...] = lax.broadcasted_iota(jnp.int32, out.shape, 1)


def live_kernel(number, count, cell, *rest):
    half = (len(rest) - 1) // 2
    rest[half][...] = jnp.where(number[...] < count[0, 0], cell[0], -1)
    for source, target in zip(rest[:half], rest[half + 1 :]):
        target[...] = source[...]


def cell_kernel(relax, pop, scell, sweight, state_o, sample_o):
    size_x, slots = pop.shape[1], scell.shape[-1]
    rates = [1.0 - jnp.broadcast_to(relax[0:1, i : i + 1], (ROWS, LANES)) for i in range(27)]
    velocity = []
    for x in range(size_x):
        density, vel, kept = relaxed([pop[i, x] for i in range(27)], rates)
        velocity.append(vel)
        for i in range(27):
            state_o[i, x] = kept[i]
        state_o[RHO, x] = density
        for d in range(3):
            state_o[VEL + d, x] = vel[d]
    sub = lax.broadcasted_iota(jnp.int32, (ROWS, LANES), 0)
    for t in range(slots // LANES):
        cells = scell[0, 0, :, t * LANES : (t + 1) * LANES]
        weights = sweight[0, 0, :, t * LANES : (t + 1) * LANES]
        row, z = cells // LANES, cells % LANES
        low = jnp.broadcast_to(z[0:1], (ROWS, LANES))
        other = z != low
        high = jnp.max(jnp.where(other, z, 0), axis=0, keepdims=True)
        high = jnp.broadcast_to(high, (ROWS, LANES))
        w_high = jnp.where(other, weights, 0.0)
        w_low = weights - w_high
        total = [None] * 3
        for x in range(size_x):
            a_low = jnp.zeros((ROWS, LANES), jnp.float32)
            a_high = a_low
            for k in range(8):
                hit = jnp.broadcast_to(row[k : k + 1], (ROWS, LANES)) == sub + x * ROWS
                a_low += jnp.where(hit, jnp.broadcast_to(w_low[k : k + 1], (ROWS, LANES)), 0.0)
                a_high += jnp.where(hit, jnp.broadcast_to(w_high[k : k + 1], (ROWS, LANES)), 0.0)
            for d in range(3):
                part = a_low * lanes_of(velocity[x][d], low) + a_high * lanes_of(velocity[x][d], high)
                total[d] = part if total[d] is None else total[d] + part
        for d in range(3):
            r = d * (slots // LANES) + t
            sample_o[r : r + 1, :] = jnp.sum(total[d], axis=0, keepdims=True)


def face_kernel(cell, normal, ref, solid, state, sample, even_o, odd_o, early_o, map_o, *, gy):
    size_x, walls = solid.shape[0], cell.shape[-1]
    row = jnp.where(cell[...] < 0, -1, cell[...] // LANES)
    z = cell[...] % LANES
    low = (ref[0] % LANES + 1).astype(jnp.float32)
    high = (ref[0] // LANES * 4 + normal[0] // 2).astype(jnp.float32)
    height = size_x * ROWS
    at = lax.broadcasted_iota(jnp.int32, (height, walls), 0) == jnp.broadcast_to(row, (height, walls))
    left = jnp.concatenate(
        [jnp.where(at, jnp.broadcast_to(v, (height, walls)), 0.0) for v in (low, high)], axis=0
    ).astype(jnp.bfloat16)
    hot = lax.broadcasted_iota(jnp.int32, (LANES, walls), 0) == jnp.broadcast_to(z, (LANES, walls))
    hot = jnp.where(hot, 1.0, 0.0).astype(jnp.bfloat16)
    dense = lax.dot_general(left, hot, (((1,), (1,)), ((), ())), preferred_element_type=jnp.float32)
    for x in range(size_x):
        low = dense[x * ROWS : (x + 1) * ROWS].astype(jnp.int32)
        high = dense[height + x * ROWS : height + (x + 1) * ROWS].astype(jnp.int32)
        map_o[REF, x] = ((high // 4) * LANES + low - 1).astype(jnp.float32)
        map_o[AXIS, x] = (high % 4).astype(jnp.float32)
        map_o[SOLID, x] = solid[x].astype(jnp.float32)
    for n in range(9):
        early_o[n] = state[18 + n, size_x - 1]
    early_o[9] = state[RHO, size_x - 1]
    early_o[10] = map_o[SOLID, size_x - 1]
    base = sample.shape[0]
    even_o[:base, :] = sample[...]
    parity = lax.axis_index(gy) % 2
    faces = []
    for b, y in ((2, ROWS - 1), (0, 0)):
        planes = [(state, direction(a, b, c)) for a in range(3) for c in range(3)]
        planes += [(state, n) for n in range(RHO, PLANES)] + [(map_o, n) for n in range(3)]
        faces.append([array[plane, x, y : y + 1, :] for array, plane in planes for x in range(size_x)])
    for n, (above, below) in enumerate(zip(*faces)):
        even_o[base + n : base + n + 1, :] = jnp.where(parity == 0, above, below)
        odd_o[n : n + 1, :] = jnp.where(parity == 0, below, above)


def first_kernel(
    cells, normal, ref, relax, solid, scell, sweight, pop, even_o, odd_o, sample_o, state_o, early_o, map_o, *, gy
):
    cell_kernel(relax, pop, scell, sweight, state_o, sample_o)
    face_kernel(cells, normal, ref, solid, state_o, sample_o, even_o, odd_o, early_o, map_o, gy=gy)


def owners(own, y_even, s_odd, far, gy, peers):
    me = lax.axis_index(gy)
    below, above = (me + peers - 1) % peers, (me + 1) % peers
    even = me % 2 == 0
    tables = [(own, me), (y_even, jnp.where(even, above, below)), (s_odd, jnp.where(even, below, above))]
    tables += [(table, (me + peers - (n + 2)) % peers) for n, table in enumerate(far)]
    return tables, me, below, above


def walled(tables, block, width, slots_each, ref, axis, vel):
    index = jnp.maximum(ref, 0)
    source = index // slots_each
    lane = block(lambda p: p * slots_each % LANES) + index % slots_each
    out = []
    for d in range(3):
        picked = jnp.zeros(ref.shape, jnp.float32)
        for table, who in tables:

            def line(p):
                return jnp.broadcast_to(table[pl.ds(d * width + p * slots_each // LANES, 1), :], (ROWS, LANES))

            picked = jnp.where(source == who, lanes_of(block(line), lane), picked)
        tangential = jnp.where(axis == d, 0.0, wall_ratio * picked)
        out.append(jnp.where(ref >= 0, tangential, vel[d]))
    return out


def beside(y_even, y_odd, gy, base, size_x):
    even = lax.axis_index(gy) % 2 == 0
    sub = lax.broadcasted_iota(jnp.int32, (ROWS, LANES), 0)

    def plane(n):
        got = (y_odd[pl.ds(n * size_x, size_x), :], y_even[pl.ds(base + n * size_x, size_x), :])
        tile = None
        for side in range(2):
            picked = jnp.where(even, got[side], got[1 - side])
            for x in range(size_x):
                row = jnp.broadcast_to(picked[x : x + 1], (ROWS, LANES))
                tile = row if tile is None else jnp.where(sub == side * size_x + x, row, tile)
        return tile

    return plane, sub


def second_kernel(own, y_even, y_odd, s_odd, state, maps, *rest, gy, peers, slots, slots_each):
    far, (plus_o, minus_o, vel_o, halo_o) = rest[: peers - 3], rest[peers - 3 :]
    size_x, width = maps.shape[1], slots // LANES
    tables, me, below, above = owners(own, y_even, s_odd, far, gy, peers)
    plane, sub = beside(y_even, y_odd, gy, up(3 * width), size_x)
    first_side = sub < size_x
    for x in range(size_x):
        ref, axis = maps[REF, x].astype(jnp.int32), maps[AXIS, x].astype(jnp.int32)
        vel = [state[VEL + d, x] for d in range(3)]
        vel = walled(tables, lambda f: f(me), width, slots_each, ref, axis, vel)
        for d in range(3):
            vel_o[d, x] = vel[d]
            if x == size_x - 1:
                plus_o[d] = vel[d]
        if x == 0:
            eq = equilibria(state[RHO, x], vel, range(9))
            for i in range(9):
                minus_o[i] = state[i, x] + eq[i]
            minus_o[9] = maps[SOLID, x]
    ref, axis = plane(13).astype(jnp.int32), plane(14).astype(jnp.int32)
    vel = [plane(10 + d) for d in range(3)]
    vel = walled(tables, lambda f: jnp.where(first_side, f(below), f(above)), width, slots_each, ref, axis, vel)
    vel[1] = jnp.where(first_side, vel[1], -vel[1])
    for d in range(3):
        halo_o[d] = vel[d]
    eq = equilibria(plane(9), vel, [direction(a, 2, c) for a in (0, 2) for c in range(3)])
    solid = plane(15)
    for o, a, x, last in ((plus_o, 2, size_x - 1, 3), (minus_o, 0, 0, 10)):
        corner = [plane(3 * a + c) + eq[direction(a, 2, c)] for c in range(3)] + [solid]
        for side in range(2):
            r = side * size_x + x
            for n in range(4):
                o[last, side * 4 + n : side * 4 + n + 1, :] = corner[n][r : r + 1]


def third_kernel(y_even, y_odd, state, vel, halo, post_o, edge_o, *, gy, slots):
    size_x = post_o.shape[1]
    plane, _ = beside(y_even, y_odd, gy, up(3 * (slots // LANES)), size_x)
    for x in range(size_x):
        eq = equilibria(state[RHO, x], [vel[d, x] for d in range(3)], range(27))
        for i in range(27):
            post_o[i, x] = state[i, x] + eq[i]
    wanted = [direction(a, 2, c) for a in range(3) for c in range(3)]
    eq = equilibria(plane(9), [halo[d] for d in range(3)], wanted)
    for n, value in enumerate([plane(n) + eq[i] for n, i in enumerate(wanted)] + [plane(15)]):
        for side in range(2):
            r = (side * 10 + n) * size_x
            edge_o[r : r + size_x, :] = value[side * size_x : (side + 1) * size_x]


def shifted(tile, row, step_y):
    if step_y == 0:
        return tile
    sub = lax.broadcasted_iota(jnp.int32, (ROWS, LANES), 0)
    rolled = pltpu.roll(tile, step_y % ROWS, 0)
    return jnp.where(sub == (0 if step_y > 0 else ROWS - 1), jnp.broadcast_to(row, (ROWS, LANES)), rolled)


def along_z(tile, c):
    return tile if c == 1 else pltpu.roll(tile, (c - 1) % LANES, 1)


def inner_kernel(post, edge, maps, out_h, out, sems):
    size_x = post.shape[1]
    copies = []
    for a in (1, 2, 0):
        first, last = max(a - 1, 0), size_x + min(a - 1, 0)
        for b in range(3):
            side = 0 if b == 2 else 1
            for x in range(first, last):
                q = x - (a - 1)

                def row(n):
                    r = (side * 10 + n) * size_x + q
                    return edge[r : r + 1, :]

                wall = shifted(maps[SOLID, q], row(9), b - 1)
                for c in range(3):
                    i = direction(a, b, c)
                    moved = along_z(shifted(post[i, q], row(3 * a + c), b - 1), c)
                    out[i, x] = jnp.where(along_z(wall, c) > 0.5, post[26 - i, x], moved)
        part = (pl.ds(9 * a, 9), pl.ds(first, last - first))
        copy = pltpu.make_async_copy(out.at[part], out_h.at[part], sems.at[a])
        copy.start()
        copies.append(copy)
    for copy in copies:
        copy.wait()


def outer_kernel(post, early, below, above, held_h, out_h, out, sems):
    del held_h
    size_x = post.shape[1]
    copies = []
    for a, x in ((0, size_x - 1), (2, 0)):
        if a == 0:
            tiles, solid, corner = [above[n] for n in range(9)], above[9], above[10]
        else:
            eq = equilibria(early[9], [below[d] for d in range(3)], range(18, 27))
            tiles, solid, corner = [early[n] + eq[18 + n] for n in range(9)], early[10], below[3]
        for b in range(3):
            side = 0 if b == 2 else 1
            wall = shifted(solid, corner[side * 4 + 3 : side * 4 + 4], b - 1)
            for c in range(3):
                i = direction(a, b, c)
                moved = shifted(tiles[3 * b + c], corner[side * 4 + c : side * 4 + c + 1], b - 1)
                moved = along_z(moved, c)
                out[i % 9 + 9 * (a // 2)] = jnp.where(along_z(wall, c) > 0.5, post[26 - i, x], moved)
        copy = pltpu.make_async_copy(out.at[pl.ds(9 * (a // 2), 9)], out_h.at[pl.ds(9 * a, 9), x], sems.at[a // 2])
        copy.start()
        copies.append(copy)
    for copy in copies:
        copy.wait()


def local(
    populations, relax, solid, wall_cell, wall_normal, wall_count, sample_ref, stencil_cell, stencil_weight
):
    _, size_x, size_y, size_z = populations.shape
    walls, slots = wall_cell.shape[-1], stencil_cell.shape[-1]
    devices, peers = lax.axis_size("gx"), lax.axis_size("gy")
    slots_each = slots // peers
    if (size_y, size_z) != (ROWS, LANES) or walls % LANES or slots % LANES:
        raise ValueError("unsupported block")
    if LANES % slots_each or peers % 2 or peers < 4 or 2 * size_x > ROWS:
        raise ValueError("unsupported mesh")
    f32 = jnp.float32
    lines = up(3 * (slots // LANES))
    face = (lines + FACE * size_x, LANES)
    block = (size_x, ROWS, LANES)
    number = pl.pallas_call(
        number_kernel,
        out_shape=jax.ShapeDtypeStruct((1, walls), jnp.int32),
        out_specs=VMEM,
        cost_estimate=pl.CostEstimate(flops=COVER, bytes_accessed=0, transcendentals=0),
        compiler_params=pltpu.CompilerParams(vmem_limit_bytes=GRANT),
        name="number",
    )()
    taken = {
        "normal": wall_normal, "ref": sample_ref, "relax": relax.reshape(1, 27),
        "solid": solid, "scell": stencil_cell, "sweight": stencil_weight,
    }
    passed = [taken[name] for name in THROUGH]
    cells, *passed = pl.pallas_call(
        live_kernel,
        out_shape=[jax.ShapeDtypeStruct(v.shape, v.dtype) for v in (number, *passed)],
        in_specs=[VMEM, pl.BlockSpec(memory_space=pltpu.SMEM)] + [VMEM] * (1 + len(passed)),
        out_specs=[VMEM] * (1 + len(passed)),
        compiler_params=pltpu.CompilerParams(vmem_limit_bytes=GRANT),
        name="live",
    )(number, wall_count, wall_cell, *passed)
    taken.update(zip(THROUGH, passed))
    y_even, y_odd, samples, state, early, maps = pl.pallas_call(
        lambda *refs: first_kernel(*refs, gy="gy"),
        out_shape=[
            jax.ShapeDtypeStruct(face, f32),
            jax.ShapeDtypeStruct((FACE * size_x, LANES), f32),
            jax.ShapeDtypeStruct((lines, LANES), f32),
            jax.ShapeDtypeStruct((PLANES, *block), f32),
            jax.ShapeDtypeStruct((11, ROWS, LANES), f32),
            jax.ShapeDtypeStruct((3, *block), f32),
        ],
        in_specs=[VMEM] * 8,
        out_specs=[VMEM] * 6,
        compiler_params=pltpu.CompilerParams(vmem_limit_bytes=GRANT),
        name="first",
    )(cells, *taken.values(), populations)

    def swap(value, odd):
        return lax.ppermute(value, "gy", [(i, (((i - odd) ^ 1) + odd) % peers) for i in range(peers)])

    got_far = []
    for n in range(2, peers - 1) if peers != 4 else ():
        got_far.append(lax.ppermute(samples, "gy", [(i, (i + n) % peers) for i in range(peers)]))
    s_odd = swap(samples, 1)
    y_odd = swap(y_odd, 1)
    y_even = swap(y_even, 0)
    if peers == 4:
        got_far = [swap(s_odd, 0)]
    ring = [(i, (i + 1) % devices) for i in range(devices)]
    early = lax.ppermute(early, "gx", ring)
    plus, minus, vel, halo = pl.pallas_call(
        lambda *refs: second_kernel(*refs, gy="gy", peers=peers, slots=slots, slots_each=slots_each),
        out_shape=[
            jax.ShapeDtypeStruct((4, ROWS, LANES), f32),
            jax.ShapeDtypeStruct((11, ROWS, LANES), f32),
            jax.ShapeDtypeStruct((3, *block), f32),
            jax.ShapeDtypeStruct((3, ROWS, LANES), f32),
        ],
        in_specs=[VMEM] * (6 + len(got_far)),
        out_specs=[VMEM] * 4,
        compiler_params=pltpu.CompilerParams(vmem_limit_bytes=GRANT),
        name="second",
    )(samples, y_even, y_odd, s_odd, state, maps, *got_far)
    post, edge = pl.pallas_call(
        lambda *refs: third_kernel(*refs, gy="gy", slots=slots),
        out_shape=[jax.ShapeDtypeStruct(populations.shape, f32), jax.ShapeDtypeStruct((up(20 * size_x), LANES), f32)],
        in_specs=[VMEM] * 5,
        out_specs=[VMEM] * 2,
        compiler_params=pltpu.CompilerParams(vmem_limit_bytes=GRANT),
        name="third",
    )(y_even, y_odd, state, vel, halo)
    from_below = lax.ppermute(plus, "gx", ring)
    from_above = lax.ppermute(minus, "gx", [(i, (i - 1) % devices) for i in range(devices)])
    held = pl.pallas_call(
        inner_kernel,
        out_shape=jax.ShapeDtypeStruct(populations.shape, f32),
        in_specs=[VMEM] * 3,
        out_specs=HBM,
        scratch_shapes=[pltpu.VMEM(populations.shape, f32), pltpu.SemaphoreType.DMA((3,))],
        compiler_params=pltpu.CompilerParams(vmem_limit_bytes=GRANT),
        name="inner",
    )(post, edge, maps)
    return pl.pallas_call(
        outer_kernel,
        out_shape=jax.ShapeDtypeStruct(populations.shape, f32),
        in_specs=[VMEM] * 4 + [HBM],
        out_specs=HBM,
        input_output_aliases={4: 0},
        scratch_shapes=[pltpu.VMEM((18, ROWS, LANES), f32), pltpu.SemaphoreType.DMA((2,))],
        compiler_params=pltpu.CompilerParams(vmem_limit_bytes=GRANT),
        name="outer",
    )(post, early, from_below, from_above, pltpu.with_memory_space_constraint(held, pltpu.HBM))


def solution(mesh):
    return jax.shard_map(
        local,
        mesh=mesh,
        in_specs=(
            P(None, "gx", "gy", None),
            P(),
            P("gx", "gy", None),
            P("gx", "gy", None),
            P("gx", "gy", None),
            P("gx", "gy"),
            P("gx", "gy", None),
            P("gx", "gy", None, None),
            P("gx", "gy", None, None),
        ),
        out_specs=P(None, "gx", "gy", None),
        check_vma=False,
    )
```

profile of v0, /device:TPU:0, one launch (start us, length us, event | category | flops | bytes accessed | tf_op | source)
XLA Modules:
  0.0 20.5 jit_solution(14101925099198535210)
XLA Ops:
  0.0 0.0 copy-start.4
  0.0 0.0 copy-start.5
  0.0 0.0 copy-start.3
  0.0 0.0 copy-start.1
  0.1 0.0 copy-start.2
  0.9 0.0 copy-done.4
  0.9 0.0 copy-done.5
  0.9 0.0 copy-done.6
  0.9 0.0 copy-done.7
  0.9 0.1 copy-done
  1.0 0.0 copy-done.3
  1.0 0.0 copy-done.1
  1.0 0.0 copy-done.2
  1.0 0.2 %first.1 = (f32[40,128]{1,0:T(8,128)S(1)}, f32[32,128]{1,0:T(8,128)S(1)}, f32[8,128]{1,0:T(8,128)S(1)}, f32[31,2,8,128]{3,2,1,0:T(8,128)S(1)}, f32[11,8,128]{2,1,0:T(8,128)S(1)}, /*index=5*/f32[3,2,8,128]{3,2,1,0:T(8,128)S(1)}) custom-call(s32[1,256]{1,0:T(1,128)S(1)} %get-tuple-element.21.refs_0_, s32[1,1,256]{2,1,0:T(1,128)S(1)} %get-tuple-element.22.refs_1_, ...), custom_call_target="tpu_custom_call" | custom-call | tf_op jit(solution)/shard_map/first/pallas_call | solution.py:404
  1.2 0.6 %collective-permute-start = (f32[40,128]{1,0:T(8,128)S(1)}, f32[40,128]{1,0:T(8,128)S(1)}, u32[]{:S(2)}, u32[]{:S(2)}) collective-permute-start(f32[40,128]{1,0:T(8,128)S(1)} %get-tuple-element.25), channel_id=1, source_target_pairs={{0,1},{1,0},{2,3},{3,2},{4,5},{5,4},{6,7},{7,6},{8,9},{9,8},{10,11... | collective-permute-start | bytes 61448 | tf_op jit(solution)/shard_map/ppermute | solution.py:421
  1.8 2.6 %collective-permute-start.1 = (f32[32,128]{1,0:T(8,128)S(1)}, f32[32,128]{1,0:T(8,128)S(1)}, u32[]{:S(2)}, u32[]{:S(2)}) collective-permute-start(f32[32,128]{1,0:T(8,128)S(1)} %get-tuple-element.26), channel_id=1, source_target_pairs={{0,3},{1,2},{2,1},{3,0},{4,7},{5,6},{6,5},{7,4},{8,11},{9,10},{10,... | collective-permute-start | bytes 49160 | tf_op jit(solution)/shard_map/ppermute | solution.py:421
  4.4 0.0 collective-permute-start.2
  4.4 3.0 %collective-permute-done.2.refs_3_ = f32[8,128]{1,0:T(8,128)S(1)} collective-permute-done((f32[8,128]{1,0:T(8,128)S(1)}, f32[8,128]{1,0:T(8,128)S(1)}, u32[]{:S(2)}, u32[]{:S(2)}) %collective-permute-start.2) | collective-permute-done | bytes 4128 | tf_op jit(solution)/shard_map/ppermute | solution.py:421
  7.4 0.1 collective-permute-start.3
  7.5 1.5 %collective-permute-start.4 = (f32[11,8,128]{2,1,0:T(8,128)S(1)}, f32[11,8,128]{2,1,0:T(8,128)S(1)}, u32[]{:S(2)}, u32[]{:S(2)}) collective-permute-start(f32[11,8,128]{2,1,0:T(8,128)S(1)} %get-tuple-element.33), channel_id=1, source_target_pairs={{0,4},{4,8},{8,12},{12,16},{16,20},{20,24},{24,28},{28,0},{1,5},{5... | collective-permute-start | bytes 135176 | tf_op jit(solution)/shard_map/ppermute | solution.py:432
  9.1 0.0 collective-permute-done.3.refs_6_
  9.1 0.0 collective-permute-done.1.refs_2_.refs_1_
  9.1 0.0 collective-permute-done.refs_1_.refs_0_
  9.1 0.1 second.1
  9.2 4.1 %collective-permute-start.6 = (f32[11,8,128]{2,1,0:T(8,128)S(1)}, f32[11,8,128]{2,1,0:T(8,128)S(1)}, u32[]{:S(2)}, u32[]{:S(2)}) collective-permute-start(f32[11,8,128]{2,1,0:T(8,128)S(1)} %get-tuple-element.35), channel_id=1, source_target_pairs={{0,28},{4,0},{8,4},{12,8},{16,12},{20,16},{24,20},{28,24},{1,29},{... | collective-permute-start | bytes 135176 | tf_op jit(solution)/shard_map/ppermute | solution.py:455
  13.3 0.0 collective-permute-start.5
  13.3 0.1 third.1
  13.4 0.8 %inner.1.held_h = f32[27,2,8,128]{3,2,1,0:T(8,128)} custom-call(f32[27,2,8,128]{3,2,1,0:T(8,128)S(1)} %get-tuple-element.32.post, f32[40,128]{1,0:T(8,128)S(1)} %get-tuple-element.36.edge, f32[3,2,8,128]{3,2,1,0:T(8,128)S(1)} %get-tuple-element.29.refs_5_.maps), custom_call_target="tpu_custom_call" | custom-call | tf_op jit(solution)/shard_map/inner/pallas_call | solution.py:456
  14.2 5.6 %collective-permute-done.5.below = f32[4,8,128]{2,1,0:T(8,128)S(1)} collective-permute-done((f32[4,8,128]{2,1,0:T(8,128)S(1)}, f32[4,8,128]{2,1,0:T(8,128)S(1)}, u32[]{:S(2)}, u32[]{:S(2)}) %collective-permute-start.5) | collective-permute-done | bytes 16416 | tf_op jit(solution)/shard_map/ppermute | solution.py:454
  19.8 0.0 collective-permute-done.4.early
  19.8 0.0 collective-permute-done.6.above
  19.8 0.7 %outer.1 = f32[27,2,8,128]{3,2,1,0:T(8,128)} custom-call(f32[27,2,8,128]{3,2,1,0:T(8,128)S(1)} %get-tuple-element.32.post, f32[11,8,128]{2,1,0:T(8,128)S(1)} %collective-permute-done.4.early, f32[4,8,128]{2,1,0:T(8,128)S(1)} %collective-permute-done.5.below, f32[11,8,128]{2,1,0:T(8,128)S(1)} %collective-permute-done.6.above, ...), custom_call_target="tpu_custom_call", output_to_operand_aliasing={{}: (4, {})} | custom-call | tf_op jit(solution)/shard_map/outer/pallas_call | solution.py:465
  (5 shorter events, 0.0 us)
Async XLA Ops:
  0.0 0.9 %copy-start.4 = (s32[1,1,256]{2,1,0:T(1,128)S(1)}, s32[1,1,256]{2,1,0:T(1,128)}, u32[]{:S(2)}) copy-start(s32[1,1,256]{2,1,0:T(1,128)} %cell.1) | copy-start | bytes 3076
  0.0 0.9 %copy-start.5 = (s32[1,1,256]{2,1,0:T(1,128)S(1)}, s32[1,1,256]{2,1,0:T(1,128)}, u32[]{:S(2)}) copy-start(s32[1,1,256]{2,1,0:T(1,128)} %rest_0_.1) | copy-start | bytes 3076
  0.0 0.9 %copy-start.6 = (s32[1,1,256]{2,1,0:T(1,128)S(1)}, s32[1,1,256]{2,1,0:T(1,128)}, u32[]{:S(2)}) copy-start(s32[1,1,256]{2,1,0:T(1,128)} %rest_1_.1) | copy-start | bytes 3076
  0.0 0.9 %copy-start.7 = (f32[27]{0:T(128)S(1)}, f32[27]{0:T(128)}, u32[]{:S(2)}) copy-start(f32[27]{0:T(128)} %param.10) | copy-start | bytes 328
  0.0 1.0 %copy-start = (f32[27,2,8,128]{3,2,1,0:T(8,128)S(1)}, f32[27,2,8,128]{3,2,1,0:T(8,128)}, u32[]{:S(2)}) copy-start(f32[27,2,8,128]{3,2,1,0:T(8,128)} %refs_7_.1) | copy-start | bytes 663556
  0.0 1.0 %copy-start.3 = (f32[1,1,8,256]{3,2,1,0:T(8,128)S(1)}, f32[1,1,8,256]{3,2,1,0:T(8,128)}, u32[]{:S(2)}) copy-start(f32[1,1,8,256]{3,2,1,0:T(8,128)} %refs_6_.1) | copy-start | bytes 24580
  0.0 1.0 %copy-start.1 = (s32[2,8,128]{2,1,0:T(8,128)S(1)}, s32[2,8,128]{2,1,0:T(8,128)}, u32[]{:S(2)}) copy-start(s32[2,8,128]{2,1,0:T(8,128)} %refs_4_.1) | copy-start | bytes 24580
  0.1 1.0 %copy-start.2 = (s32[1,1,8,256]{3,2,1,0:T(8,128)S(1)}, s32[1,1,8,256]{3,2,1,0:T(8,128)}, u32[]{:S(2)}) copy-start(s32[1,1,8,256]{3,2,1,0:T(8,128)} %refs_5_.1) | copy-start | bytes 24580
  1.2 7.8 %collective-permute-start = (f32[40,128]{1,0:T(8,128)S(1)}, f32[40,128]{1,0:T(8,128)S(1)}, u32[]{:S(2)}, u32[]{:S(2)}) collective-permute-start(f32[40,128]{1,0:T(8,128)S(1)} %get-tuple-element.25), channel_id=1, source_target_pairs={{0,1},{1,0},{2,3},{3,2},{4,5},{5,4},{6,7},{7,6},{8,9},{9,8},{10,11... | collective-permute-start | bytes 61448 | tf_op jit(solution)/shard_map/ppermute | solution.py:421
  1.8 7.3 %collective-permute-start.1 = (f32[32,128]{1,0:T(8,128)S(1)}, f32[32,128]{1,0:T(8,128)S(1)}, u32[]{:S(2)}, u32[]{:S(2)}) collective-permute-start(f32[32,128]{1,0:T(8,128)S(1)} %get-tuple-element.26), channel_id=1, source_target_pairs={{0,3},{1,2},{2,1},{3,0},{4,7},{5,6},{6,5},{7,4},{8,11},{9,10},{10,... | collective-permute-start | bytes 49160 | tf_op jit(solution)/shard_map/ppermute | solution.py:421
  4.4 3.0 %collective-permute-start.2 = (f32[8,128]{1,0:T(8,128)S(1)}, f32[8,128]{1,0:T(8,128)S(1)}, u32[]{:S(2)}, u32[]{:S(2)}) collective-permute-start(f32[8,128]{1,0:T(8,128)S(1)} %get-tuple-element.28.refs_0_), channel_id=1, source_target_pairs={{0,3},{1,2},{2,1},{3,0},{4,7},{5,6},{6,5},{7,4},{8,11},{9,10},{10,... | collective-permute-start | bytes 12296 | tf_op jit(solution)/shard_map/ppermute | solution.py:421
  7.4 1.6 %collective-permute-start.3 = (f32[8,128]{1,0:T(8,128)S(1)}, f32[8,128]{1,0:T(8,128)S(1)}, u32[]{:S(2)}, u32[]{:S(2)}) collective-permute-start(f32[8,128]{1,0:T(8,128)S(1)} %collective-permute-done.2.refs_3_), channel_id=1, source_target_pairs={{0,1},{1,0},{2,3},{3,2},{4,5},{5,4},{6,7},{7,6},{8,9},{9,8},{10,11... | collective-permute-start | bytes 12296 | tf_op jit(solution)/shard_map/ppermute | solution.py:421
  7.5 12.3 %collective-permute-start.4 = (f32[11,8,128]{2,1,0:T(8,128)S(1)}, f32[11,8,128]{2,1,0:T(8,128)S(1)}, u32[]{:S(2)}, u32[]{:S(2)}) collective-permute-start(f32[11,8,128]{2,1,0:T(8,128)S(1)} %get-tuple-element.33), channel_id=1, source_target_pairs={{0,4},{4,8},{8,12},{12,16},{16,20},{20,24},{24,28},{28,0},{1,5},{5... | collective-permute-start | bytes 135176 | tf_op jit(solution)/shard_map/ppermute | solution.py:432
  9.2 10.6 %collective-permute-start.6 = (f32[11,8,128]{2,1,0:T(8,128)S(1)}, f32[11,8,128]{2,1,0:T(8,128)S(1)}, u32[]{:S(2)}, u32[]{:S(2)}) collective-permute-start(f32[11,8,128]{2,1,0:T(8,128)S(1)} %get-tuple-element.35), channel_id=1, source_target_pairs={{0,28},{4,0},{8,4},{12,8},{16,12},{20,16},{24,20},{28,24},{1,29},{... | collective-permute-start | bytes 135176 | tf_op jit(solution)/shard_map/ppermute | solution.py:455
  13.3 6.4 %collective-permute-start.5 = (f32[4,8,128]{2,1,0:T(8,128)S(1)}, f32[4,8,128]{2,1,0:T(8,128)S(1)}, u32[]{:S(2)}, u32[]{:S(2)}) collective-permute-start(f32[4,8,128]{2,1,0:T(8,128)S(1)} %get-tuple-element.34), channel_id=1, source_target_pairs={{0,4},{4,8},{8,12},{12,16},{16,20},{20,24},{24,28},{28,0},{1,5},{5... | collective-permute-start | bytes 49160 | tf_op jit(solution)/shard_map/ppermute | solution.py:454
where the time goes:
time: 20.7 us; the launch traced here: 20.5 us
  starting transfers between devices  8.95 us (43%)
  waiting for transfers between devices  8.58 us (41%)
  Pallas kernels  1.96 us (9%)
  between operations  0.91 us (4%)
    ppermute x1, waiting for transfers between devices, local(): from_below = lax.ppermute(plus, 'gx', ring)  5.57 us
    ppermute x1, starting transfers between devices, local(): lax.ppermute(minus, 'gx', [(i, (i - 1) % devices) for i in range(devices)])  4.13 us
    ppermute x4, starting transfers between devices, swap(): lax.ppermute(value, 'gy', [(i, ((i - odd ^ 1) + odd) % peers) for i in ra...  3.3 us
    ppermute x4, waiting for transfers between devices, swap(): lax.ppermute(value, 'gy', [(i, ((i - odd ^ 1) + odd) % peers) for i in ra...  3 us
    ppermute x1, starting transfers between devices, local(): early = lax.ppermute(early, 'gx', ring)  1.52 us
    pallas_call x1, Pallas kernels, local(): pl.pallas_call(inner_kernel, out_shape=jax.ShapeDtypeStruct(populations.s...  0.78 us
    pallas_call x1, Pallas kernels, local(): pl.pallas_call(outer_kernel, out_shape=jax.ShapeDtypeStruct(populations.s...  0.73 us
  transfers between devices with their start and end apart: 7, of which 2 were waited for; matrix products, arithmetic and copies ran while one was open for 0% of the time, Pallas kernels for 5%

commit v1 on v0

--- a/solution.py
+++ b/solution.py
@@ -188,6 +188,7 @@
     early_o[10] = map_o[SOLID, size_x - 1]
     base = sample.shape[0]
     even_o[:base, :] = sample[...]
+    odd_o[:base, :] = sample[...]
     parity = lax.axis_index(gy) % 2
     faces = []
     for b, y in ((2, ROWS - 1), (0, 0)):
@@ -196,7 +197,7 @@
         faces.append([array[plane, x, y : y + 1, :] for array, plane in planes for x in range(size_x)])
     for n, (above, below) in enumerate(zip(*faces)):
         even_o[base + n : base + n + 1, :] = jnp.where(parity == 0, above, below)
-        odd_o[n : n + 1, :] = jnp.where(parity == 0, below, above)
+        odd_o[base + n : base + n + 1, :] = jnp.where(parity == 0, below, above)
 
 
 def first_kernel(
@@ -206,11 +207,11 @@
     face_kernel(cells, normal, ref, solid, state_o, sample_o, even_o, odd_o, early_o, map_o, gy=gy)
 
 
-def owners(own, y_even, s_odd, far, gy, peers):
+def owners(own, y_even, y_odd, far, gy, peers):
     me = lax.axis_index(gy)
     below, above = (me + peers - 1) % peers, (me + 1) % peers
     even = me % 2 == 0
-    tables = [(own, me), (y_even, jnp.where(even, above, below)), (s_odd, jnp.where(even, below, above))]
+    tables = [(own, me), (y_even, jnp.where(even, above, below)), (y_odd, jnp.where(even, below, above))]
     tables += [(table, (me + peers - (n + 2)) % peers) for n, table in enumerate(far)]
     return tables, me, below, above
 
@@ -238,7 +239,8 @@
     sub = lax.broadcasted_iota(jnp.int32, (ROWS, LANES), 0)
 
     def plane(n):
-        got = (y_odd[pl.ds(n * size_x, size_x), :], y_even[pl.ds(base + n * size_x, size_x), :])
+        rows = pl.ds(base + n * size_x, size_x)
+        got = (y_odd[rows, :], y_even[rows, :])
         tile = None
         for side in range(2):
             picked = jnp.where(even, got[side], got[1 - side])
@@ -250,10 +252,10 @@
     return plane, sub
 
 
-def second_kernel(own, y_even, y_odd, s_odd, state, maps, *rest, gy, peers, slots, slots_each):
+def second_kernel(own, y_even, y_odd, state, maps, *rest, gy, peers, slots, slots_each):
     far, (plus_o, minus_o, vel_o, halo_o) = rest[: peers - 3], rest[peers - 3 :]
     size_x, width = maps.shape[1], slots // LANES
-    tables, me, below, above = owners(own, y_even, s_odd, far, gy, peers)
+    tables, me, below, above = owners(own, y_even, y_odd, far, gy, peers)
     plane, sub = beside(y_even, y_odd, gy, up(3 * width), size_x)
     first_side = sub < size_x
     for x in range(size_x):
@@ -405,7 +407,7 @@
         lambda *refs: first_kernel(*refs, gy="gy"),
         out_shape=[
             jax.ShapeDtypeStruct(face, f32),
-            jax.ShapeDtypeStruct((FACE * size_x, LANES), f32),
+            jax.ShapeDtypeStruct(face, f32),
             jax.ShapeDtypeStruct((lines, LANES), f32),
             jax.ShapeDtypeStruct((PLANES, *block), f32),
             jax.ShapeDtypeStruct((11, ROWS, LANES), f32),
@@ -423,11 +425,10 @@
     got_far = []
     for n in range(2, peers - 1) if peers != 4 else ():
         got_far.append(lax.ppermute(samples, "gy", [(i, (i + n) % peers) for i in range(peers)]))
-    s_odd = swap(samples, 1)
     y_odd = swap(y_odd, 1)
     y_even = swap(y_even, 0)
     if peers == 4:
-        got_far = [swap(s_odd, 0)]
+        got_far = [swap(y_odd, 0)]
     ring = [(i, (i + 1) % devices) for i in range(devices)]
     early = lax.ppermute(early, "gx", ring)
     plus, minus, vel, halo = pl.pallas_call(
@@ -438,11 +439,11 @@
             jax.ShapeDtypeStruct((3, *block), f32),
             jax.ShapeDtypeStruct((3, ROWS, LANES), f32),
         ],
-        in_specs=[VMEM] * (6 + len(got_far)),
+        in_specs=[VMEM] * (5 + len(got_far)),
         out_specs=[VMEM] * 4,
         compiler_params=pltpu.CompilerParams(vmem_limit_bytes=GRANT),
         name="second",
-    )(samples, y_even, y_odd, s_odd, state, maps, *got_far)
+    )(samples, y_even, y_odd, state, maps, *got_far)
     post, edge = pl.pallas_call(
         lambda *refs: third_kernel(*refs, gy="gy", slots=slots),
         out_shape=[jax.ShapeDtypeStruct(populations.shape, f32), jax.ShapeDtypeStruct((up(20 * size_x), LANES), f32)],

time: 20.7 us -> 19.4 us (0.937)
  waiting for transfers between devices: 8.58 us -> 6.42 us
  starting transfers between devices: 8.95 us -> 9.87 us
    ppermute x4 -> x3, waiting for transfers between devices: 3 us -> 0.85 us  [swap(): lax.ppermute(value, 'gy', [(i, ((i - odd ^ 1) + odd) % peers) for i in ra...]
    ppermute x4 -> x3, starting transfers between devices: 3.3 us -> 3.77 us  [swap(): lax.ppermute(value, 'gy', [(i, ((i - odd ^ 1) + odd) % peers) for i in ra...]
    ppermute x1, starting transfers between devices: 1.52 us -> 1.94 us  [local(): early = lax.ppermute(early, 'gx', ring)]
  transfers between devices with their start and end apart: 7 -> 6, of which waited for: 2 -> 3; matrix products, arithmetic and copies ran while one was open for 0% -> 0% of each run, Pallas kernels for 5% -> 5%
where the time goes in v1:
time: 19.4 us; the launch traced here: 19.3 us
  starting transfers between devices  9.87 us (51%)
  waiting for transfers between devices  6.42 us (33%)
  Pallas kernels  1.96 us (10%)
  between operations  0.9 us (5%)
    ppermute x1, waiting for transfers between devices, local(): from_below = lax.ppermute(plus, 'gx', ring)  5.49 us
    ppermute x1, starting transfers between devices, local(): lax.ppermute(minus, 'gx', [(i, (i - 1) % devices) for i in range(devices)])  4.16 us
    ppermute x3, starting transfers between devices, swap(): lax.ppermute(value, 'gy', [(i, ((i - odd ^ 1) + odd) % peers) for i in ra...  3.77 us
    ppermute x1, starting transfers between devices, local(): early = lax.ppermute(early, 'gx', ring)  1.94 us
    ppermute x3, waiting for transfers between devices, swap(): lax.ppermute(value, 'gy', [(i, ((i - odd ^ 1) + odd) % peers) for i in ra...  0.85 us
    pallas_call x1, Pallas kernels, local(): pl.pallas_call(inner_kernel, out_shape=jax.ShapeDtypeStruct(populations.s...  0.78 us
    pallas_call x1, Pallas kernels, local(): pl.pallas_call(outer_kernel, out_shape=jax.ShapeDtypeStruct(populations.s...  0.73 us
  transfers between devices with their start and end apart: 6, of which 3 were waited for; matrix products, arithmetic and copies ran while one was open for 0% of the time, Pallas kernels for 5%

profile of v1, /device:TPU:0, one launch (start us, length us, event | category | flops | bytes accessed | tf_op | source)
XLA Modules:
  0.0 19.3 jit_solution(1222050496463318938)
XLA Ops:
  0.0 0.0 copy-start.4
  0.0 0.0 copy-start.5
  0.0 0.0 copy-start.6
  0.0 0.0 copy-start.7
  0.0 0.0 copy-start.3
  0.0 0.0 copy-start.1
  0.1 0.0 copy-start.2
  0.9 0.0 copy-done.4
  0.9 0.0 copy-done.5
  0.9 0.0 copy-done.6
  0.9 0.0 copy-done.7
  0.9 0.1 copy-done
  1.0 0.0 copy-done.3
  1.0 0.0 copy-done.1
  1.0 0.0 copy-done.2
  1.0 0.2 %first.1 = (f32[40,128]{1,0:T(8,128)S(1)}, f32[40,128]{1,0:T(8,128)S(1)}, f32[8,128]{1,0:T(8,128)S(1)}, f32[31,2,8,128]{3,2,1,0:T(8,128)S(1)}, f32[11,8,128]{2,1,0:T(8,128)S(1)}, /*index=5*/f32[3,2,8,128]{3,2,1,0:T(8,128)S(1)}) custom-call(s32[1,256]{1,0:T(1,128)S(1)} %get-tuple-element.21.refs_0_, s32[1,1,256]{2,1,0:T(1,128)S(1)} %get-tuple-element.22.refs_1_, ...), custom_call_target="tpu_custom_call" | custom-call | tf_op jit(solution)/shard_map/first/pallas_call | solution.py:406
  1.2 2.5 %collective-permute-start.1 = (f32[40,128]{1,0:T(8,128)S(1)}, f32[40,128]{1,0:T(8,128)S(1)}, u32[]{:S(2)}, u32[]{:S(2)}) collective-permute-start(f32[40,128]{1,0:T(8,128)S(1)} %get-tuple-element.26), channel_id=1, source_target_pairs={{0,3},{1,2},{2,1},{3,0},{4,7},{5,6},{6,5},{7,4},{8,11},{9,10},{10,... | collective-permute-start | bytes 61448 | tf_op jit(solution)/shard_map/ppermute | solution.py:423
  3.7 0.7 %collective-permute-start = (f32[40,128]{1,0:T(8,128)S(1)}, f32[40,128]{1,0:T(8,128)S(1)}, u32[]{:S(2)}, u32[]{:S(2)}) collective-permute-start(f32[40,128]{1,0:T(8,128)S(1)} %get-tuple-element.25), channel_id=1, source_target_pairs={{0,1},{1,0},{2,3},{3,2},{4,5},{5,4},{6,7},{7,6},{8,9},{9,8},{10,11... | collective-permute-start | bytes 61448 | tf_op jit(solution)/shard_map/ppermute | solution.py:423
  4.4 0.8 %collective-permute-done.1.refs_2_.refs_1_ = f32[40,128]{1,0:T(8,128)S(1)} collective-permute-done((f32[40,128]{1,0:T(8,128)S(1)}, f32[40,128]{1,0:T(8,128)S(1)}, u32[]{:S(2)}, u32[]{:S(2)}) %collective-permute-start.1) | collective-permute-done | bytes 20512 | tf_op jit(solution)/shard_map/ppermute | solution.py:423
  5.2 0.6 %collective-permute-start.2 = (f32[40,128]{1,0:T(8,128)S(1)}, f32[40,128]{1,0:T(8,128)S(1)}, u32[]{:S(2)}, u32[]{:S(2)}) collective-permute-start(f32[40,128]{1,0:T(8,128)S(1)} %collective-permute-done.1.refs_2_.refs_1_), channel_id=1, source_target_pairs={{0,1},{1,0},{2,3},{3,2},{4,5},{5,4},{6,7},{7,6},{8,9},{9,8},{10,11... | collective-permute-start | bytes 61448 | tf_op jit(solution)/shard_map/ppermute | solution.py:423
  5.9 1.9 %collective-permute-start.3 = (f32[11,8,128]{2,1,0:T(8,128)S(1)}, f32[11,8,128]{2,1,0:T(8,128)S(1)}, u32[]{:S(2)}, u32[]{:S(2)}) collective-permute-start(f32[11,8,128]{2,1,0:T(8,128)S(1)} %get-tuple-element.33), channel_id=1, source_target_pairs={{0,4},{4,8},{8,12},{12,16},{16,20},{20,24},{24,28},{28,0},{1,5},{5... | collective-permute-start | bytes 135176 | tf_op jit(solution)/shard_map/ppermute | solution.py:433
  7.8 0.0 collective-permute-done.refs_1_.refs_0_
  7.8 0.0 collective-permute-done.2.refs_5_
  7.8 0.1 second.1
  7.9 4.2 %collective-permute-start.5 = (f32[11,8,128]{2,1,0:T(8,128)S(1)}, f32[11,8,128]{2,1,0:T(8,128)S(1)}, u32[]{:S(2)}, u32[]{:S(2)}) collective-permute-start(f32[11,8,128]{2,1,0:T(8,128)S(1)} %get-tuple-element.35), channel_id=1, source_target_pairs={{0,28},{4,0},{8,4},{12,8},{16,12},{20,16},{24,20},{28,24},{1,29},{... | collective-permute-start | bytes 135176 | tf_op jit(solution)/shard_map/ppermute | solution.py:456
  12.1 0.0 collective-permute-start.4
  12.1 0.1 third.1
  12.2 0.8 %inner.1.held_h = f32[27,2,8,128]{3,2,1,0:T(8,128)} custom-call(f32[27,2,8,128]{3,2,1,0:T(8,128)S(1)} %get-tuple-element.32.post, f32[40,128]{1,0:T(8,128)S(1)} %get-tuple-element.36.edge, f32[3,2,8,128]{3,2,1,0:T(8,128)S(1)} %get-tuple-element.29.refs_4_.maps), custom_call_target="tpu_custom_call" | custom-call | tf_op jit(solution)/shard_map/inner/pallas_call | solution.py:457
  13.0 0.1 collective-permute-done.3.early
  13.0 5.5 %collective-permute-done.4.below = f32[4,8,128]{2,1,0:T(8,128)S(1)} collective-permute-done((f32[4,8,128]{2,1,0:T(8,128)S(1)}, f32[4,8,128]{2,1,0:T(8,128)S(1)}, u32[]{:S(2)}, u32[]{:S(2)}) %collective-permute-start.4) | collective-permute-done | bytes 16416 | tf_op jit(solution)/shard_map/ppermute | solution.py:455
  18.5 0.0 collective-permute-done.5.above
  18.5 0.7 %outer.1 = f32[27,2,8,128]{3,2,1,0:T(8,128)} custom-call(f32[27,2,8,128]{3,2,1,0:T(8,128)S(1)} %get-tuple-element.32.post, f32[11,8,128]{2,1,0:T(8,128)S(1)} %collective-permute-done.3.early, f32[4,8,128]{2,1,0:T(8,128)S(1)} %collective-permute-done.4.below, f32[11,8,128]{2,1,0:T(8,128)S(1)} %collective-permute-done.5.above, ...), custom_call_target="tpu_custom_call", output_to_operand_aliasing={{}: (4, {})} | custom-call | tf_op jit(solution)/shard_map/outer/pallas_call | solution.py:466
  (3 shorter events, 0.0 us)
Async XLA Ops:
  0.0 0.9 %copy-start.4 = (s32[1,1,256]{2,1,0:T(1,128)S(1)}, s32[1,1,256]{2,1,0:T(1,128)}, u32[]{:S(2)}) copy-start(s32[1,1,256]{2,1,0:T(1,128)} %cell.1) | copy-start | bytes 3076
  0.0 0.9 %copy-start.5 = (s32[1,1,256]{2,1,0:T(1,128)S(1)}, s32[1,1,256]{2,1,0:T(1,128)}, u32[]{:S(2)}) copy-start(s32[1,1,256]{2,1,0:T(1,128)} %rest_0_.1) | copy-start | bytes 3076
  0.0 0.9 %copy-start.6 = (s32[1,1,256]{2,1,0:T(1,128)S(1)}, s32[1,1,256]{2,1,0:T(1,128)}, u32[]{:S(2)}) copy-start(s32[1,1,256]{2,1,0:T(1,128)} %rest_1_.1) | copy-start | bytes 3076
  0.0 0.9 %copy-start.7 = (f32[27]{0:T(128)S(1)}, f32[27]{0:T(128)}, u32[]{:S(2)}) copy-start(f32[27]{0:T(128)} %param.10) | copy-start | bytes 328
  0.0 1.0 %copy-start = (f32[27,2,8,128]{3,2,1,0:T(8,128)S(1)}, f32[27,2,8,128]{3,2,1,0:T(8,128)}, u32[]{:S(2)}) copy-start(f32[27,2,8,128]{3,2,1,0:T(8,128)} %refs_7_.1) | copy-start | bytes 663556
  0.0 1.0 %copy-start.3 = (f32[1,1,8,256]{3,2,1,0:T(8,128)S(1)}, f32[1,1,8,256]{3,2,1,0:T(8,128)}, u32[]{:S(2)}) copy-start(f32[1,1,8,256]{3,2,1,0:T(8,128)} %refs_6_.1) | copy-start | bytes 24580
  0.0 1.0 %copy-start.1 = (s32[2,8,128]{2,1,0:T(8,128)S(1)}, s32[2,8,128]{2,1,0:T(8,128)}, u32[]{:S(2)}) copy-start(s32[2,8,128]{2,1,0:T(8,128)} %refs_4_.1) | copy-start | bytes 24580
  0.1 1.0 %copy-start.2 = (s32[1,1,8,256]{3,2,1,0:T(8,128)S(1)}, s32[1,1,8,256]{3,2,1,0:T(8,128)}, u32[]{:S(2)}) copy-start(s32[1,1,8,256]{3,2,1,0:T(8,128)} %refs_5_.1) | copy-start | bytes 24580
  1.2 4.0 %collective-permute-start.1 = (f32[40,128]{1,0:T(8,128)S(1)}, f32[40,128]{1,0:T(8,128)S(1)}, u32[]{:S(2)}, u32[]{:S(2)}) collective-permute-start(f32[40,128]{1,0:T(8,128)S(1)} %get-tuple-element.26), channel_id=1, source_target_pairs={{0,3},{1,2},{2,1},{3,0},{4,7},{5,6},{6,5},{7,4},{8,11},{9,10},{10,... | collective-permute-start | bytes 61448 | tf_op jit(solution)/shard_map/ppermute | solution.py:423
  3.7 4.1 %collective-permute-start = (f32[40,128]{1,0:T(8,128)S(1)}, f32[40,128]{1,0:T(8,128)S(1)}, u32[]{:S(2)}, u32[]{:S(2)}) collective-permute-start(f32[40,128]{1,0:T(8,128)S(1)} %get-tuple-element.25), channel_id=1, source_target_pairs={{0,1},{1,0},{2,3},{3,2},{4,5},{5,4},{6,7},{7,6},{8,9},{9,8},{10,11... | collective-permute-start | bytes 61448 | tf_op jit(solution)/shard_map/ppermute | solution.py:423
  5.2 2.6 %collective-permute-start.2 = (f32[40,128]{1,0:T(8,128)S(1)}, f32[40,128]{1,0:T(8,128)S(1)}, u32[]{:S(2)}, u32[]{:S(2)}) collective-permute-start(f32[40,128]{1,0:T(8,128)S(1)} %collective-permute-done.1.refs_2_.refs_1_), channel_id=1, source_target_pairs={{0,1},{1,0},{2,3},{3,2},{4,5},{5,4},{6,7},{7,6},{8,9},{9,8},{10,11... | collective-permute-start | bytes 61448 | tf_op jit(solution)/shard_map/ppermute | solution.py:423
  5.9 7.2 %collective-permute-start.3 = (f32[11,8,128]{2,1,0:T(8,128)S(1)}, f32[11,8,128]{2,1,0:T(8,128)S(1)}, u32[]{:S(2)}, u32[]{:S(2)}) collective-permute-start(f32[11,8,128]{2,1,0:T(8,128)S(1)} %get-tuple-element.33), channel_id=1, source_target_pairs={{0,4},{4,8},{8,12},{12,16},{16,20},{20,24},{24,28},{28,0},{1,5},{5... | collective-permute-start | bytes 135176 | tf_op jit(solution)/shard_map/ppermute | solution.py:433
  7.9 10.6 %collective-permute-start.5 = (f32[11,8,128]{2,1,0:T(8,128)S(1)}, f32[11,8,128]{2,1,0:T(8,128)S(1)}, u32[]{:S(2)}, u32[]{:S(2)}) collective-permute-start(f32[11,8,128]{2,1,0:T(8,128)S(1)} %get-tuple-element.35), channel_id=1, source_target_pairs={{0,28},{4,0},{8,4},{12,8},{16,12},{20,16},{24,20},{28,24},{1,29},{... | collective-permute-start | bytes 135176 | tf_op jit(solution)/shard_map/ppermute | solution.py:456
  12.1 6.4 %collective-permute-start.4 = (f32[4,8,128]{2,1,0:T(8,128)S(1)}, f32[4,8,128]{2,1,0:T(8,128)S(1)}, u32[]{:S(2)}, u32[]{:S(2)}) collective-permute-start(f32[4,8,128]{2,1,0:T(8,128)S(1)} %get-tuple-element.34), channel_id=1, source_target_pairs={{0,4},{4,8},{8,12},{12,16},{16,20},{20,24},{24,28},{28,0},{1,5},{5... | collective-permute-start | bytes 49160 | tf_op jit(solution)/shard_map/ppermute | solution.py:455

commit v2 on v0

--- a/solution.py
+++ b/solution.py
@@ -357,9 +357,9 @@
                 moved = shifted(tiles[3 * b + c], corner[side * 4 + c : side * 4 + c + 1], b - 1)
                 moved = along_z(moved, c)
                 out[i % 9 + 9 * (a // 2)] = jnp.where(along_z(wall, c) > 0.5, post[26 - i, x], moved)
-        copy = pltpu.make_async_copy(out.at[pl.ds(9 * (a // 2), 9)], out_h.at[pl.ds(9 * a, 9), x], sems.at[a // 2])
-        copy.start()
-        copies.append(copy)
+            held, taken = out.at[pl.ds(9 * (a // 2) + 3 * b, 3)], out_h.at[pl.ds(9 * a + 3 * b, 3), x]
+            copies.append(pltpu.make_async_copy(held, taken, sems.at[len(copies)]))
+            copies[-1].start()
     for copy in copies:
         copy.wait()
 
@@ -468,7 +468,7 @@
         in_specs=[VMEM] * 4 + [HBM],
         out_specs=HBM,
         input_output_aliases={4: 0},
-        scratch_shapes=[pltpu.VMEM((18, ROWS, LANES), f32), pltpu.SemaphoreType.DMA((2,))],
+        scratch_shapes=[pltpu.VMEM((18, ROWS, LANES), f32), pltpu.SemaphoreType.DMA((6,))],
         compiler_params=pltpu.CompilerParams(vmem_limit_bytes=GRANT),
         name="outer",
     )(post, early, from_below, from_above, pltpu.with_memory_space_constraint(held, pltpu.HBM))

time: 20.7 us -> 20.7 us (level)
  no operation moved by 1% of the time
where the time goes in v2:
time: 20.7 us; the launch traced here: 20.5 us
  starting transfers between devices  8.95 us (43%)
  waiting for transfers between devices  8.58 us (41%)
  Pallas kernels  1.98 us (10%)
  between operations  0.91 us (4%)
    ppermute x1, waiting for transfers between devices, local(): from_below = lax.ppermute(plus, 'gx', ring)  5.57 us
    ppermute x1, starting transfers between devices, local(): lax.ppermute(minus, 'gx', [(i, (i - 1) % devices) for i in range(devices)])  4.13 us
    ppermute x4, starting transfers between devices, swap(): lax.ppermute(value, 'gy', [(i, ((i - odd ^ 1) + odd) % peers) for i in ra...  3.3 us
    ppermute x4, waiting for transfers between devices, swap(): lax.ppermute(value, 'gy', [(i, ((i - odd ^ 1) + odd) % peers) for i in ra...  3 us
    ppermute x1, starting transfers between devices, local(): early = lax.ppermute(early, 'gx', ring)  1.52 us
    pallas_call x1, Pallas kernels, local(): pl.pallas_call(inner_kernel, out_shape=jax.ShapeDtypeStruct(populations.s...  0.78 us
    pallas_call x1, Pallas kernels, local(): pl.pallas_call(outer_kernel, out_shape=jax.ShapeDtypeStruct(populations.s...  0.75 us
  transfers between devices with their start and end apart: 7, of which 2 were waited for; matrix products, arithmetic and copies ran while one was open for 0% of the time, Pallas kernels for 5%

profile of v2, /device:TPU:0, one launch (start us, length us, event | category | flops | bytes accessed | tf_op | source)
XLA Modules:
  0.0 20.5 jit_solution(4553182850993567972)
XLA Ops:
  0.0 0.0 copy-start.4
  0.0 0.0 copy-start.5
  0.0 0.0 copy-start.3
  0.0 0.0 copy-start.1
  0.1 0.0 copy-start.2
  0.9 0.0 copy-done.4
  0.9 0.0 copy-done.5
  0.9 0.0 copy-done.6
  0.9 0.0 copy-done.7
  0.9 0.1 copy-done
  1.0 0.0 copy-done.3
  1.0 0.0 copy-done.1
  1.0 0.0 copy-done.2
  1.0 0.2 %first.1 = (f32[40,128]{1,0:T(8,128)S(1)}, f32[32,128]{1,0:T(8,128)S(1)}, f32[8,128]{1,0:T(8,128)S(1)}, f32[31,2,8,128]{3,2,1,0:T(8,128)S(1)}, f32[11,8,128]{2,1,0:T(8,128)S(1)}, /*index=5*/f32[3,2,8,128]{3,2,1,0:T(8,128)S(1)}) custom-call(s32[1,256]{1,0:T(1,128)S(1)} %get-tuple-element.21.refs_0_, s32[1,1,256]{2,1,0:T(1,128)S(1)} %get-tuple-element.22.refs_1_, ...), custom_call_target="tpu_custom_call" | custom-call | tf_op jit(solution)/shard_map/first/pallas_call | solution.py:404
  1.2 0.6 %collective-permute-start = (f32[40,128]{1,0:T(8,128)S(1)}, f32[40,128]{1,0:T(8,128)S(1)}, u32[]{:S(2)}, u32[]{:S(2)}) collective-permute-start(f32[40,128]{1,0:T(8,128)S(1)} %get-tuple-element.25), channel_id=1, source_target_pairs={{0,1},{1,0},{2,3},{3,2},{4,5},{5,4},{6,7},{7,6},{8,9},{9,8},{10,11... | collective-permute-start | bytes 61448 | tf_op jit(solution)/shard_map/ppermute | solution.py:421
  1.8 2.6 %collective-permute-start.1 = (f32[32,128]{1,0:T(8,128)S(1)}, f32[32,128]{1,0:T(8,128)S(1)}, u32[]{:S(2)}, u32[]{:S(2)}) collective-permute-start(f32[32,128]{1,0:T(8,128)S(1)} %get-tuple-element.26), channel_id=1, source_target_pairs={{0,3},{1,2},{2,1},{3,0},{4,7},{5,6},{6,5},{7,4},{8,11},{9,10},{10,... | collective-permute-start | bytes 49160 | tf_op jit(solution)/shard_map/ppermute | solution.py:421
  4.4 0.0 collective-permute-start.2
  4.4 3.0 %collective-permute-done.2.refs_3_ = f32[8,128]{1,0:T(8,128)S(1)} collective-permute-done((f32[8,128]{1,0:T(8,128)S(1)}, f32[8,128]{1,0:T(8,128)S(1)}, u32[]{:S(2)}, u32[]{:S(2)}) %collective-permute-start.2) | collective-permute-done | bytes 4128 | tf_op jit(solution)/shard_map/ppermute | solution.py:421
  7.4 0.1 collective-permute-start.3
  7.5 1.5 %collective-permute-start.4 = (f32[11,8,128]{2,1,0:T(8,128)S(1)}, f32[11,8,128]{2,1,0:T(8,128)S(1)}, u32[]{:S(2)}, u32[]{:S(2)}) collective-permute-start(f32[11,8,128]{2,1,0:T(8,128)S(1)} %get-tuple-element.33), channel_id=1, source_target_pairs={{0,4},{4,8},{8,12},{12,16},{16,20},{20,24},{24,28},{28,0},{1,5},{5... | collective-permute-start | bytes 135176 | tf_op jit(solution)/shard_map/ppermute | solution.py:432
  9.1 0.0 collective-permute-done.3.refs_6_
  9.1 0.0 collective-permute-done.1.refs_2_.refs_1_
  9.1 0.0 collective-permute-done.refs_1_.refs_0_
  9.1 0.1 second.1
  9.2 4.1 %collective-permute-start.6 = (f32[11,8,128]{2,1,0:T(8,128)S(1)}, f32[11,8,128]{2,1,0:T(8,128)S(1)}, u32[]{:S(2)}, u32[]{:S(2)}) collective-permute-start(f32[11,8,128]{2,1,0:T(8,128)S(1)} %get-tuple-element.35), channel_id=1, source_target_pairs={{0,28},{4,0},{8,4},{12,8},{16,12},{20,16},{24,20},{28,24},{1,29},{... | collective-permute-start | bytes 135176 | tf_op jit(solution)/shard_map/ppermute | solution.py:455
  13.3 0.0 collective-permute-start.5
  13.3 0.1 third.1
  13.4 0.8 %inner.1.held_h = f32[27,2,8,128]{3,2,1,0:T(8,128)} custom-call(f32[27,2,8,128]{3,2,1,0:T(8,128)S(1)} %get-tuple-element.32.post, f32[40,128]{1,0:T(8,128)S(1)} %get-tuple-element.36.edge, f32[3,2,8,128]{3,2,1,0:T(8,128)S(1)} %get-tuple-element.29.refs_5_.maps), custom_call_target="tpu_custom_call" | custom-call | tf_op jit(solution)/shard_map/inner/pallas_call | solution.py:456
  14.2 5.6 %collective-permute-done.5.below = f32[4,8,128]{2,1,0:T(8,128)S(1)} collective-permute-done((f32[4,8,128]{2,1,0:T(8,128)S(1)}, f32[4,8,128]{2,1,0:T(8,128)S(1)}, u32[]{:S(2)}, u32[]{:S(2)}) %collective-permute-start.5) | collective-permute-done | bytes 16416 | tf_op jit(solution)/shard_map/ppermute | solution.py:454
  19.8 0.0 collective-permute-done.4.early
  19.8 0.0 collective-permute-done.6.above
  19.8 0.8 %outer.1 = f32[27,2,8,128]{3,2,1,0:T(8,128)} custom-call(f32[27,2,8,128]{3,2,1,0:T(8,128)S(1)} %get-tuple-element.32.post, f32[11,8,128]{2,1,0:T(8,128)S(1)} %collective-permute-done.4.early, f32[4,8,128]{2,1,0:T(8,128)S(1)} %collective-permute-done.5.below, f32[11,8,128]{2,1,0:T(8,128)S(1)} %collective-permute-done.6.above, ...), custom_call_target="tpu_custom_call", output_to_operand_aliasing={{}: (4, {})} | custom-call | tf_op jit(solution)/shard_map/outer/pallas_call | solution.py:465
  (5 shorter events, 0.0 us)
Async XLA Ops:
  0.0 0.9 %copy-start.4 = (s32[1,1,256]{2,1,0:T(1,128)S(1)}, s32[1,1,256]{2,1,0:T(1,128)}, u32[]{:S(2)}) copy-start(s32[1,1,256]{2,1,0:T(1,128)} %cell.1) | copy-start | bytes 3076
  0.0 0.9 %copy-start.5 = (s32[1,1,256]{2,1,0:T(1,128)S(1)}, s32[1,1,256]{2,1,0:T(1,128)}, u32[]{:S(2)}) copy-start(s32[1,1,256]{2,1,0:T(1,128)} %rest_0_.1) | copy-start | bytes 3076
  0.0 0.9 %copy-start.6 = (s32[1,1,256]{2,1,0:T(1,128)S(1)}, s32[1,1,256]{2,1,0:T(1,128)}, u32[]{:S(2)}) copy-start(s32[1,1,256]{2,1,0:T(1,128)} %rest_1_.1) | copy-start | bytes 3076
  0.0 0.9 %copy-start.7 = (f32[27]{0:T(128)S(1)}, f32[27]{0:T(128)}, u32[]{:S(2)}) copy-start(f32[27]{0:T(128)} %param.10) | copy-start | bytes 328
  0.0 1.0 %copy-start = (f32[27,2,8,128]{3,2,1,0:T(8,128)S(1)}, f32[27,2,8,128]{3,2,1,0:T(8,128)}, u32[]{:S(2)}) copy-start(f32[27,2,8,128]{3,2,1,0:T(8,128)} %refs_7_.1) | copy-start | bytes 663556
  0.0 1.0 %copy-start.3 = (f32[1,1,8,256]{3,2,1,0:T(8,128)S(1)}, f32[1,1,8,256]{3,2,1,0:T(8,128)}, u32[]{:S(2)}) copy-start(f32[1,1,8,256]{3,2,1,0:T(8,128)} %refs_6_.1) | copy-start | bytes 24580
  0.0 1.0 %copy-start.1 = (s32[2,8,128]{2,1,0:T(8,128)S(1)}, s32[2,8,128]{2,1,0:T(8,128)}, u32[]{:S(2)}) copy-start(s32[2,8,128]{2,1,0:T(8,128)} %refs_4_.1) | copy-start | bytes 24580
  0.1 1.0 %copy-start.2 = (s32[1,1,8,256]{3,2,1,0:T(8,128)S(1)}, s32[1,1,8,256]{3,2,1,0:T(8,128)}, u32[]{:S(2)}) copy-start(s32[1,1,8,256]{3,2,1,0:T(8,128)} %refs_5_.1) | copy-start | bytes 24580
  1.2 7.8 %collective-permute-start = (f32[40,128]{1,0:T(8,128)S(1)}, f32[40,128]{1,0:T(8,128)S(1)}, u32[]{:S(2)}, u32[]{:S(2)}) collective-permute-start(f32[40,128]{1,0:T(8,128)S(1)} %get-tuple-element.25), channel_id=1, source_target_pairs={{0,1},{1,0},{2,3},{3,2},{4,5},{5,4},{6,7},{7,6},{8,9},{9,8},{10,11... | collective-permute-start | bytes 61448 | tf_op jit(solution)/shard_map/ppermute | solution.py:421
  1.8 7.3 %collective-permute-start.1 = (f32[32,128]{1,0:T(8,128)S(1)}, f32[32,128]{1,0:T(8,128)S(1)}, u32[]{:S(2)}, u32[]{:S(2)}) collective-permute-start(f32[32,128]{1,0:T(8,128)S(1)} %get-tuple-element.26), channel_id=1, source_target_pairs={{0,3},{1,2},{2,1},{3,0},{4,7},{5,6},{6,5},{7,4},{8,11},{9,10},{10,... | collective-permute-start | bytes 49160 | tf_op jit(solution)/shard_map/ppermute | solution.py:421
  4.4 3.0 %collective-permute-start.2 = (f32[8,128]{1,0:T(8,128)S(1)}, f32[8,128]{1,0:T(8,128)S(1)}, u32[]{:S(2)}, u32[]{:S(2)}) collective-permute-start(f32[8,128]{1,0:T(8,128)S(1)} %get-tuple-element.28.refs_0_), channel_id=1, source_target_pairs={{0,3},{1,2},{2,1},{3,0},{4,7},{5,6},{6,5},{7,4},{8,11},{9,10},{10,... | collective-permute-start | bytes 12296 | tf_op jit(solution)/shard_map/ppermute | solution.py:421
  7.4 1.6 %collective-permute-start.3 = (f32[8,128]{1,0:T(8,128)S(1)}, f32[8,128]{1,0:T(8,128)S(1)}, u32[]{:S(2)}, u32[]{:S(2)}) collective-permute-start(f32[8,128]{1,0:T(8,128)S(1)} %collective-permute-done.2.refs_3_), channel_id=1, source_target_pairs={{0,1},{1,0},{2,3},{3,2},{4,5},{5,4},{6,7},{7,6},{8,9},{9,8},{10,11... | collective-permute-start | bytes 12296 | tf_op jit(solution)/shard_map/ppermute | solution.py:421
  7.5 12.3 %collective-permute-start.4 = (f32[11,8,128]{2,1,0:T(8,128)S(1)}, f32[11,8,128]{2,1,0:T(8,128)S(1)}, u32[]{:S(2)}, u32[]{:S(2)}) collective-permute-start(f32[11,8,128]{2,1,0:T(8,128)S(1)} %get-tuple-element.33), channel_id=1, source_target_pairs={{0,4},{4,8},{8,12},{12,16},{16,20},{20,24},{24,28},{28,0},{1,5},{5... | collective-permute-start | bytes 135176 | tf_op jit(solution)/shard_map/ppermute | solution.py:432
  9.2 10.6 %collective-permute-start.6 = (f32[11,8,128]{2,1,0:T(8,128)S(1)}, f32[11,8,128]{2,1,0:T(8,128)S(1)}, u32[]{:S(2)}, u32[]{:S(2)}) collective-permute-start(f32[11,8,128]{2,1,0:T(8,128)S(1)} %get-tuple-element.35), channel_id=1, source_target_pairs={{0,28},{4,0},{8,4},{12,8},{16,12},{20,16},{24,20},{28,24},{1,29},{... | collective-permute-start | bytes 135176 | tf_op jit(solution)/shard_map/ppermute | solution.py:455
  13.3 6.4 %collective-permute-start.5 = (f32[4,8,128]{2,1,0:T(8,128)S(1)}, f32[4,8,128]{2,1,0:T(8,128)S(1)}, u32[]{:S(2)}, u32[]{:S(2)}) collective-permute-start(f32[4,8,128]{2,1,0:T(8,128)S(1)} %get-tuple-element.34), channel_id=1, source_target_pairs={{0,4},{4,8},{8,12},{12,16},{16,20},{20,24},{24,28},{28,0},{1,5},{5... | collective-permute-start | bytes 49160 | tf_op jit(solution)/shard_map/ppermute | solution.py:454
